TPU v7x, 32 devices: a whole 2x2x4 slice. The times are simulated.
32 devices in a mesh: shard: 4 (over y, x), replica: 8 (over z, core).
Axes of the slice: x: 2, y: 2, z: 4, core: 2. Of those that a mesh axis runs over, the one named last changes fastest.
Arguments:
- tokens: bfloat16 [8192, 1536], P(('shard', 'replica')), may hold values from -6 to 6
- cotangent: bfloat16 [8192, 1536], P(('shard', 'replica')), may hold values from -6 to 6
- seq_lengths: int32 [64], replicated, may hold values from 0 to 256, as said below
- seq_device: int32 [64], replicated, may hold values from 0 to 31
- seq_offsets: int32 [64], replicated, may hold values from 0 to 1
- norm_attn: bfloat16 [1, 1536], P(None, 'shard'), may hold values from 0.5 to 1.5
- w_qkv: bfloat16 [1, 1536, 3072], P(None, 'shard'), may hold values from -0.15625 to 0.15625
- w_out: bfloat16 [1, 1536, 1536], P(None, 'shard'), may hold values from -0.625 to 0.625
- norm_mlp: bfloat16 [1, 1536], P(None, 'shard'), may hold values from 0.5 to 1.5
- w_gate_up: bfloat16 [1, 1536, 8192], P(None, 'shard'), may hold values from -0.15625 to 0.15625
- w_down: bfloat16 [1, 4096, 1536], P(None, 'shard'), may hold values from -0.125 to 0.125
Outputs:
- result: bfloat16 [8192, 1536], P(('shard', 'replica'))
- grad_tokens: float32 [8192, 1536], P(('shard', 'replica'))
- grad_norm_attn: float32 [1, 1536], P(None, 'shard')
- grad_w_qkv: float32 [1, 1536, 3072], P(None, 'shard')
- grad_w_out: float32 [1, 1536, 1536], P(None, 'shard')
- grad_norm_mlp: float32 [1, 1536], P(None, 'shard')
- grad_w_gate_up: float32 [1, 1536, 8192], P(None, 'shard')
- grad_w_down: float32 [1, 4096, 1536], P(None, 'shard')
Inputs may be any that keep to these rules, and one draw needn't show every extreme that they name: `seq_lengths`: each device is named by exactly 2 entries. A sequence lies within blocks 2p and 2p + 1 of its device for some p; sequences of one device never share a row; length 0 marks an unused entry. In every draw some device is full, its every pair of blocks holding one sequence of length 256.
All inputs are finite; a program needn't handle non-finite values.
Results may differ from a plain program's by a relative error of at most 0.02.
Values may be sent and summed in bfloat16 or wider, within the bound.
A program may use at most 320 MiB of HBM per device.

v0:
```python
import jax
import jax.numpy as jnp
from jax import lax
from jax.sharding import PartitionSpec as P

HEADS = 16
KV_HEADS = 8
HEAD = 96
FF = 4096
BLOCK = 128
epsilon = 1e-05
rope_base = 100000.0


def rms_scale(field):
    return lax.rsqrt(jnp.mean(field * field, axis=-1, keepdims=True) + epsilon)


def rotate(field):
    half = field.shape[-1] // 2
    return jnp.concatenate([-field[..., half:], field[..., :half]], axis=-1)


def rope_tables(position):
    half = HEAD // 2
    freqs = rope_base ** (-(jnp.arange(half, dtype=jnp.float32) * 2.0) / HEAD)
    angles = position.astype(jnp.float32)[:, None] * freqs[None, :]
    cosine = jnp.cos(angles)
    sine = jnp.sin(angles)
    return (jnp.concatenate([cosine, cosine], axis=-1), jnp.concatenate([sine, sine], axis=-1))


def locate(device, seq_lengths, seq_device, seq_offsets, rows):
    starts = seq_offsets * BLOCK
    local = jnp.arange(rows, dtype=jnp.int32)
    labels = jnp.arange(seq_lengths.shape[0], dtype=jnp.int32)
    hits = (
        (seq_device[None, :] == device)
        & (local[:, None] >= starts[None, :])
        & (local[:, None] < (starts + seq_lengths)[None, :])
    )
    segment = jnp.max(jnp.where(hits, labels[None, :], -1), axis=1)
    begin = jnp.sum(jnp.where(hits, starts[None, :], 0), axis=1)
    return (segment, local - begin)


def mask_of(segment):
    local = jnp.arange(segment.shape[0], dtype=jnp.int32)
    return (segment[:, None] == segment[None, :]) & (local[None, :] <= local[:, None])


def contract_rows(left, right):
    return lax.dot_general(
        left, right, (((0,), (0,)), ((), ())), preferred_element_type=jnp.float32
    )


def contract_cols(left, right):
    return lax.dot_general(
        left, right, (((1,), (1,)), ((), ())), preferred_element_type=jnp.float32
    )


def norm_rows(field, gain):
    scale = rms_scale(field)
    normed = (field * scale * gain.astype(jnp.float32)[None, :]).astype(jnp.bfloat16)
    return (scale, normed)


def norm_back(grad_normed, field, scale, gain):
    normed = field * scale
    grad_gain = jnp.sum(grad_normed * normed, axis=0)
    inner = grad_normed * gain[None, :]
    grad_field = scale * (inner - normed * jnp.mean(inner * normed, axis=-1, keepdims=True))
    return (grad_field, grad_gain)


def split_project(project, q_heads, k_heads, cosine, sine):
    rows = project.shape[0]
    width_q = q_heads * HEAD
    width_k = k_heads * HEAD
    queries = project[:, :width_q].reshape(rows, q_heads, HEAD)
    keys = project[:, width_q : width_q + width_k].reshape(rows, k_heads, HEAD)
    values_b = project[:, width_q + width_k :].reshape(rows, k_heads, HEAD).astype(jnp.bfloat16)
    queries_b = (queries * cosine[:, None, :] + rotate(queries) * sine[:, None, :]).astype(
        jnp.bfloat16
    )
    keys_b = (keys * cosine[:, None, :] + rotate(keys) * sine[:, None, :]).astype(jnp.bfloat16)
    return (queries_b, keys_b, values_b)


def join_grads(grad_queries, grad_keys, grad_values, cosine, sine):
    rows = grad_queries.shape[0]
    grad_queries = grad_queries * cosine[:, None, :] - rotate(grad_queries * sine[:, None, :])
    grad_keys = grad_keys * cosine[:, None, :] - rotate(grad_keys * sine[:, None, :])
    return jnp.concatenate(
        [
            grad_queries.reshape(rows, -1),
            grad_keys.reshape(rows, -1),
            grad_values.reshape(rows, -1),
        ],
        axis=1,
    ).astype(jnp.bfloat16)


def attention_scores(queries_b, keys_b, allowed):
    rows = queries_b.shape[0]
    kv_count = keys_b.shape[1]
    grouped = queries_b.reshape(rows, kv_count, queries_b.shape[1] // kv_count, HEAD)
    scores = jnp.einsum(
        "qkgd,pkd->kgqp", grouped, keys_b, preferred_element_type=jnp.float32
    ) * HEAD ** (-0.5)
    return jnp.where(allowed, scores, -1e30)


def attend_forward(queries_b, keys_b, values_b, allowed):
    rows = queries_b.shape[0]
    scores = attention_scores(queries_b, keys_b, allowed)
    top = jnp.max(scores, axis=-1, keepdims=True)
    total = jnp.log(jnp.sum(jnp.exp(scores - top), axis=-1, keepdims=True)) + top
    weights_b = jnp.exp(scores - total).astype(jnp.bfloat16)
    mixed = jnp.einsum("kgqp,pkd->qkgd", weights_b, values_b, preferred_element_type=jnp.float32)
    return (mixed.reshape(rows, -1).astype(jnp.bfloat16), total)


def attend_backward(grad_mixed_b, queries_b, keys_b, values_b, total, allowed):
    rows = queries_b.shape[0]
    q_heads = queries_b.shape[1]
    kv_count = keys_b.shape[1]
    per = q_heads // kv_count
    factor = HEAD ** (-0.5)
    grad_mixed = grad_mixed_b.reshape(rows, kv_count, per, HEAD)
    weights = jnp.exp(attention_scores(queries_b, keys_b, allowed) - total)
    weights_b = weights.astype(jnp.bfloat16)
    grad_values = jnp.einsum(
        "kgqp,qkgd->pkd", weights_b, grad_mixed, preferred_element_type=jnp.float32
    )
    grad_weights = jnp.einsum(
        "qkgd,pkd->kgqp", grad_mixed, values_b, preferred_element_type=jnp.float32
    )
    grad_scores = weights * (grad_weights - jnp.sum(weights * grad_weights, axis=-1, keepdims=True))
    grad_scores_b = grad_scores.astype(jnp.bfloat16)
    grouped = queries_b.reshape(rows, kv_count, per, HEAD)
    grad_queries = jnp.einsum(
        "kgqp,pkd->qkgd", grad_scores_b, keys_b, preferred_element_type=jnp.float32
    )
    grad_queries = grad_queries.reshape(rows, q_heads, HEAD) * factor
    grad_keys = (
        jnp.einsum("kgqp,qkgd->pkd", grad_scores_b, grouped, preferred_element_type=jnp.float32)
        * factor
    )
    return (grad_queries, grad_keys, grad_values)


def gate_back(grad_hidden, gate_up, local_ff):
    gate = gate_up[:, :local_ff]
    upper = gate_up[:, local_ff:]
    sigma = jax.nn.sigmoid(gate)
    grad_gate = grad_hidden * upper * sigma * (1.0 + gate * (1.0 - sigma))
    grad_upper = grad_hidden * (gate * sigma)
    return jnp.concatenate([grad_gate, grad_upper], axis=1).astype(jnp.bfloat16)


def attention_forward(field, gain, w_project, w_output, allowed, cosine, sine):
    scale, normed = norm_rows(field, gain)
    project = jnp.dot(normed, w_project, preferred_element_type=jnp.float32)
    queries_b, keys_b, values_b = split_project(project, HEADS, KV_HEADS, cosine, sine)
    mixed, total = attend_forward(queries_b, keys_b, values_b, allowed)
    after = field + jnp.dot(mixed, w_output, preferred_element_type=jnp.float32)
    return (after, (scale, normed, queries_b, keys_b, values_b, total, mixed))


def attention_backward(grad_field, field, gain, w_project, w_output, saved, allowed, cosine, sine):
    scale, normed, queries_b, keys_b, values_b, total, mixed = saved
    grad_branch = grad_field.astype(jnp.bfloat16)
    grad_w_output = contract_rows(mixed, grad_branch)
    grad_mixed = contract_cols(grad_branch, w_output).astype(jnp.bfloat16)
    grad_queries, grad_keys, grad_values = attend_backward(
        grad_mixed, queries_b, keys_b, values_b, total, allowed
    )
    grad_project = join_grads(grad_queries, grad_keys, grad_values, cosine, sine)
    grad_w_project = contract_rows(normed, grad_project)
    grad_normed = contract_cols(grad_project, w_project)
    grad_input, grad_gain = norm_back(grad_normed, field, scale, gain.astype(jnp.float32))
    return (grad_field + grad_input, grad_gain, grad_w_project, grad_w_output)


def mlp_forward(field, gain, w_gateup, w_lower):
    scale, normed = norm_rows(field, gain)
    gate_up = jnp.dot(normed, w_gateup, preferred_element_type=jnp.float32)
    hidden = (jax.nn.silu(gate_up[:, :FF]) * gate_up[:, FF:]).astype(jnp.bfloat16)
    after = field + jnp.dot(hidden, w_lower, preferred_element_type=jnp.float32)
    return (after, (scale, normed, gate_up, hidden))


def mlp_backward(grad_field, field, gain, w_gateup, w_lower, saved):
    scale, normed, gate_up, hidden = saved
    grad_branch = grad_field.astype(jnp.bfloat16)
    grad_w_lower = contract_rows(hidden, grad_branch)
    grad_hidden = contract_cols(grad_branch, w_lower)
    grad_gateup = gate_back(grad_hidden, gate_up, FF)
    grad_w_gateup = contract_rows(normed, grad_gateup)
    grad_normed = contract_cols(grad_gateup, w_gateup)
    grad_input, grad_gain = norm_back(grad_normed, field, scale, gain.astype(jnp.float32))
    return (grad_field + grad_input, grad_gain, grad_w_gateup, grad_w_lower)


def settle(owned):
    return (
        lax.psum(owned[0].astype(jnp.bfloat16), "replica").astype(jnp.float32),
        lax.psum(owned[1].astype(jnp.bfloat16), "replica").astype(jnp.float32),
        lax.psum(owned[2].astype(jnp.bfloat16), "replica").astype(jnp.float32),
        lax.psum(owned[3].astype(jnp.bfloat16), "replica").astype(jnp.float32),
        lax.psum(owned[4].astype(jnp.bfloat16), "replica").astype(jnp.float32),
        lax.psum(owned[5].astype(jnp.bfloat16), "replica").astype(jnp.float32),
    )


def body(
    tokens,
    cotangent,
    seq_lengths,
    seq_device,
    seq_offsets,
    norm_attn,
    w_qkv,
    w_out,
    norm_mlp,
    w_gate_up,
    w_down,
):
    rows = tokens.shape[0]
    layers = w_qkv.shape[0]
    device = lax.axis_index(("shard", "replica"))
    segment, position = locate(device, seq_lengths, seq_device, seq_offsets, rows)
    live = (segment >= 0).astype(jnp.float32)[:, None]
    field = tokens.astype(jnp.float32)
    per_layer = [None] * layers
    cosine, sine = rope_tables(position)
    allowed = mask_of(segment)
    layer = 0
    attn_parts = (
        lax.all_gather(norm_attn[layer], "shard", axis=0, tiled=True),
        lax.all_gather(w_qkv[layer], "shard", axis=0, tiled=True),
        lax.all_gather(w_out[layer], "shard", axis=0, tiled=True),
    )
    middle, attn_saved = attention_forward(
        field, attn_parts[0], attn_parts[1], attn_parts[2], allowed, cosine, sine
    )
    mlp_parts = (
        lax.all_gather(norm_mlp[layer], "shard", axis=0, tiled=True),
        lax.all_gather(w_gate_up[layer], "shard", axis=0, tiled=True),
        lax.all_gather(w_down[layer], "shard", axis=0, tiled=True),
    )
    after, mlp_saved = mlp_forward(middle, mlp_parts[0], mlp_parts[1], mlp_parts[2])
    kept_inputs = [(field, attn_saved, middle, mlp_saved)]
    result = (after * live).astype(jnp.bfloat16)
    grad_field = cotangent.astype(jnp.float32) * live
    for layer in reversed(range(layers)):
        field_in, attn_saved, middle, mlp_saved = kept_inputs[layer]
        mlp_parts = (
            lax.all_gather(norm_mlp[layer], "shard", axis=0, tiled=True),
            lax.all_gather(w_gate_up[layer], "shard", axis=0, tiled=True),
            lax.all_gather(w_down[layer], "shard", axis=0, tiled=True),
        )
        grad_middle, grad_gain_mlp, grad_gateup, grad_lower = mlp_backward(
            grad_field, middle, mlp_parts[0], mlp_parts[1], mlp_parts[2], mlp_saved
        )
        mlp_owned = (
            lax.psum_scatter(
                grad_gain_mlp.astype(jnp.bfloat16), "shard", scatter_dimension=0, tiled=True
            ).astype(jnp.float32),
            lax.psum_scatter(
                grad_gateup.astype(jnp.bfloat16), "shard", scatter_dimension=0, tiled=True
            ).astype(jnp.float32),
            lax.psum_scatter(
                grad_lower.astype(jnp.bfloat16), "shard", scatter_dimension=0, tiled=True
            ).astype(jnp.float32),
        )
        attn_parts = (
            lax.all_gather(norm_attn[layer], "shard", axis=0, tiled=True),
            lax.all_gather(w_qkv[layer], "shard", axis=0, tiled=True),
            lax.all_gather(w_out[layer], "shard", axis=0, tiled=True),
        )
        grad_field, grad_gain_attn, grad_project, grad_output = attention_backward(
            grad_middle,
            field_in,
            attn_parts[0],
            attn_parts[1],
            attn_parts[2],
            attn_saved,
            allowed,
            cosine,
            sine,
        )
        attn_owned = (
            lax.psum_scatter(
                grad_gain_attn.astype(jnp.bfloat16), "shard", scatter_dimension=0, tiled=True
            ).astype(jnp.float32),
            lax.psum_scatter(
                grad_project.astype(jnp.bfloat16), "shard", scatter_dimension=0, tiled=True
            ).astype(jnp.float32),
            lax.psum_scatter(
                grad_output.astype(jnp.bfloat16), "shard", scatter_dimension=0, tiled=True
            ).astype(jnp.float32),
        )
        per_layer[layer] = settle(
            (attn_owned[0], attn_owned[1], attn_owned[2], mlp_owned[0], mlp_owned[1], mlp_owned[2])
        )
    stacked = [jnp.stack([entry[member] for entry in per_layer], axis=0) for member in range(6)]
    return (
        result,
        grad_field,
        stacked[0],
        stacked[1],
        stacked[2],
        stacked[3],
        stacked[4],
        stacked[5],
    )


def solution(mesh):
    placed = (
        P(("shard", "replica"), None),
        P(("shard", "replica"), None),
        P(),
        P(),
        P(),
        P(None, "shard"),
        P(None, "shard", None),
        P(None, "shard", None),
        P(None, "shard"),
        P(None, "shard", None),
        P(None, "shard", None),
    )
    return jax.shard_map(
        body,
        mesh=mesh,
        in_specs=placed,
        out_specs=(
            P(("shard", "replica"), None),
            P(("shard", "replica"), None),
            P(None, "shard"),
            P(None, "shard", None),
            P(None, "shard", None),
            P(None, "shard"),
            P(None, "shard", None),
            P(None, "shard", None),
        ),
        check_vma=False,
    )
```

profile of v0, /device:TPU:0, one launch (start us, length us, event | category | flops | bytes accessed | tf_op | source)
XLA Modules:
  0.0 1345.5 jit_solution(480248952729375393)
XLA Ops:
  10.1 9.6 all-gather
  19.7 8.2 all-gather.3
  30.7 78.1 %all-gather.11.cloned.1.call-done = bf16[1,1536,3072]{2,1,0:T(8,128)(2,1)} async-done(((bf16[1,384,3072]{2,1,0:T(8,128)(2,1)}), bf16[1,1536,3072]{2,1,0:T(8,128)(2,1)}) %all-gather.11.cloned.1.call-update) | async-done | bytes 9437200 | tf_op jit(solution)/shard_map/all_gather | solution.py:244
  108.8 5.2 fusion.10
  125.3 42.3 %all-gather.13.cloned.1.call-done = bf16[1,1536,1536]{2,1,0:T(8,128)(2,1)} async-done(((bf16[1,384,1536]{2,1,0:T(8,128)(2,1)}), bf16[1,1536,1536]{2,1,0:T(8,128)(2,1)}) %all-gather.13.cloned.1.call-update) | async-done | bytes 4718608 | tf_op jit(solution)/shard_map/all_gather | solution.py:245
  171.4 225.6 %all-gather.15.cloned.1.call-done = bf16[1,1536,8192]{2,1,0:T(8,128)(2,1)} async-done(((bf16[1,384,8192]{2,1,0:T(8,128)(2,1)}), bf16[1,1536,8192]{2,1,0:T(8,128)(2,1)}) %all-gather.15.cloned.1.call-update) | async-done | bytes 25165840 | tf_op jit(solution)/shard_map/all_gather | solution.py:252
  397.1 13.8 %fusion.2 = f32[256,8192]{1,0:T(8,128)} fusion(bf16[1,1536,8192]{2,1,0:T(8,128)(2,1)} %all-gather.15.cloned.1.call-done, f32[256,1536]{1,0:T(8,128)S(1)} %get-tuple-element.44, f32[1536]{0:T(1024)S(1)} %convert_reduce_fusion, f32[256]{0:T(256)S(1)} %add_rsqrt_fusion), kind=kOutput, calls=%fused_computation.3 | convolution fusion | flops 6443630592 | bytes 35134464 | tf_op jit(solution)/shard_map/dot_general | solution.py:190
  410.9 110.3 %all-gather.17.cloned.1.call-done = bf16[1,4096,1536]{2,1,0:T(8,128)(2,1)} async-done(((bf16[1,1024,1536]{2,1,0:T(8,128)(2,1)}), bf16[1,4096,1536]{2,1,0:T(8,128)(2,1)}) %all-gather.17.cloned.1.call-update) | async-done | bytes 12582928 | tf_op jit(solution)/shard_map/all_gather | solution.py:253
  521.2 10.4 multiply_convert_fusion.1
  531.6 14.9 %multiply_reduce_fusion = (bf16[1536]{0:T(1024)(128)(2,1)}, f32[256]{0:T(256)S(1)}, f32[256,1536]{1,0:T(8,128)}) fusion(f32[256,1536]{1,0:T(8,128)S(1)} %get-tuple-element.44, f32[256]{0:T(256)S(1)} %add_rsqrt_fusion, f32[1536]{0:T(1024)S(1)} %convert_reduce_fusion, bf16[1,1536,8192]{2,1,0:T(8,128)(2,1)} %all-gather.15.cloned.1.call-done, ...), kind=kOutput, calls=%fused_computation.63 | convolution fusion | flops 6453196800 | bytes 32517120 | tf_op jit(solution)/shard_map/dot_general | solution.py:59
  552.2 4.6 fusion.33
  570.9 7.3 convolution_convert_fusion.2
  578.3 10.2 convolution_convert_fusion.1
  588.5 14.2 %convolution_convert_fusion = bf16[1536,8192]{1,0:T(8,128)(2,1)} fusion(bf16[256,4096]{1,0:T(8,128)(2,1)} %copy-done.16, bf16[256,4096]{1,0:T(8,128)(2,1)} %copy-done.15, f32[256,1536]{1,0:T(8,128)S(1)} %get-tuple-element.44, f32[1536]{0:T(1024)S(1)} %convert_reduce_fusion, f32[256]{0:T(256)} %copy-done.27), kind=kOutput, calls=%fused_computation | convolution fusion | flops 6464602112 | bytes 30940160 | tf_op jit(solution)/shard_map/dot_general | solution.py:53
  603.0 6.2 reduce-scatter.7.cloned.1.call-done
  609.2 97.9 %reduce-scatter.5.cloned.1.call-done = bf16[384,3072]{1,0:T(8,128)(2,1)} async-done(((bf16[1536,3072]{1,0:T(8,128)(2,1)}), bf16[384,3072]{1,0:T(8,128)(2,1)}) %reduce-scatter.5.cloned.1.call-update) | async-done | bytes 2359312 | tf_op jit(solution)/shard_map/reduce_scatter | solution.py:300
  707.1 124.3 %reduce-scatter.11.cloned.1.call-done = bf16[1024,1536]{1,0:T(8,128)(2,1)} async-done(((bf16[4096,1536]{1,0:T(8,128)(2,1)}), bf16[1024,1536]{1,0:T(8,128)(2,1)}) %reduce-scatter.11.cloned.1.call-update) | async-done | bytes 3145744 | tf_op jit(solution)/shard_map/reduce_scatter | solution.py:276
  831.4 224.9 %reduce-scatter.9.cloned.1.call-done = bf16[384,8192]{1,0:T(8,128)(2,1)} async-done(((bf16[1536,8192]{1,0:T(8,128)(2,1)}), bf16[384,8192]{1,0:T(8,128)(2,1)}) %reduce-scatter.9.cloned.1.call-update) | async-done | bytes 6291472 | tf_op jit(solution)/shard_map/reduce_scatter | solution.py:273
  1058.2 8.8 fusion.46
  1067.0 9.2 all-reduce.4
  1076.4 15.4 %all-reduce.2 = (bf16[1,384]{1,0:T(2,128)(2,1)S(1)}, bf16[1,384]{1,0:T(2,128)(2,1)S(1)}) all-reduce(bf16[1,384]{1,0:T(2,128)(2,1)S(1)} %stack.36, bf16[1,384]{1,0:T(2,128)(2,1)S(1)} %stack.42), channel_id=1, replica_groups=mesh['shard'=4,'replica'=8] {'replica'}, use_global_device_ids=true, to_apply=%region_11.12 | all-reduce | flops 768 | bytes 3072 | tf_op jit(solution)/shard_map/psum | solution.py:210
  1096.9 9.0 fusion.30
  1105.9 215.4 %all-reduce.7.cloned.1.call-done = (bf16[1,384,3072]{2,1,0:T(8,128)(2,1)}, bf16[1,384,1536]{2,1,0:T(8,128)(2,1)}, bf16[1,384,8192]{2,1,0:T(8,128)(2,1)}, bf16[1,1024,1536]{2,1,0:T(8,128)(2,1)}) async-done(((bf16[1,384,3072]{2,1,0:T(8,128)(2,1)}, bf16[1,384,1536]{2,1,0:T(8,128)(2,1)}, bf16[1,384,8192]{2,1,0:T(8,128)(2,1)}, bf16[1,1024,1536]{2,1,0:T(8,128)(2,1)}), (bf16[1,384,3072]{2,1,0:T(8,128)(2,1)}, ...) | async-done | bytes 12976144 | tf_op jit(solution)/shard_map/psum | solution.py:211
  1328.8 6.3 stack.45
  (156 shorter events, 58.1 us)
Async XLA Ops:
  7.2 101.6 %all-gather.11.cloned.1.call-start = ((), (), s32[]{:S(2)}) async-start(), calls=%async_computation.8 | async-start | bytes 11796480 | tf_op jit(solution)/shard_map/all_gather | solution.py:244
  7.9 159.7 %all-gather.13.cloned.1.call-start = ((), (), s32[]{:S(2)}) async-start(), calls=%async_computation.9 | async-start | bytes 5898240 | tf_op jit(solution)/shard_map/all_gather | solution.py:245
  8.7 388.4 %all-gather.15.cloned.1.call-start = ((), (), s32[]{:S(2)}) async-start(), calls=%async_computation.10 | async-start | bytes 31457280 | tf_op jit(solution)/shard_map/all_gather | solution.py:252
  9.4 10.3 copy-start.36
  9.4 18.5 %copy-start.39 = (s32[64]{0:T(128)S(1)}, s32[64]{0:T(128)}, u32[]{:S(2)}) copy-start(s32[64]{0:T(128)} %param.14) | copy-start | bytes 772
  9.4 18.6 %copy-start.37 = (s32[64]{0:T(128)S(1)}, s32[64]{0:T(128)}, u32[]{:S(2)}) copy-start(s32[64]{0:T(128)} %param.15) | copy-start | bytes 772
  9.4 18.6 %copy-start.38 = (s32[64]{0:T(128)S(1)}, s32[64]{0:T(128)}, u32[]{:S(2)}) copy-start(s32[64]{0:T(128)} %param.13) | copy-start | bytes 772
  9.4 19.7 %copy-start.2 = (bf16[256,1536]{1,0:T(8,128)(2,1)S(1)}, bf16[256,1536]{1,0:T(8,128)(2,1)}, u32[]{:S(2)}) copy-start(bf16[256,1536]{1,0:T(8,128)(2,1)} %param.11) | copy-start | bytes 2359300
  9.4 511.8 %all-gather.17.cloned.1.call-start = ((), (), s32[]{:S(2)}) async-start(), calls=%async_computation.11 | async-start | bytes 15728640 | tf_op jit(solution)/shard_map/all_gather | solution.py:253
  10.0 599.2 %reduce-scatter.7.cloned.1.call-start = ((), (), s32[]{:S(2)}) async-start(), calls=%async_computation.5 | async-start | bytes 5898240 | tf_op jit(solution)/shard_map/reduce_scatter | solution.py:303
  29.4 84.6 %copy-start.28 = (f32[256]{0:T(256)}, f32[256]{0:T(256)S(1)}, u32[]{:S(2)}) copy-start(f32[256]{0:T(256)S(1)} %add_rsqrt_fusion.1) | copy-start | bytes 3076
  125.3 46.1 %copy-start.4 = (bf16[8,96,2,256]{3,1,2,0:T(8,128)(2,1)}, bf16[8,96,2,256]{3,1,2,0:T(8,128)(2,1)S(1)}, u32[]{:S(2)}) copy-start(bf16[8,96,2,256]{3,1,2,0:T(8,128)(2,1)S(1)} %convolution_convert_fusion.4) | copy-start | bytes 2359300
  171.4 360.2 %copy-start.27 = (f32[256]{0:T(256)}, f32[256]{0:T(256)S(1)}, u32[]{:S(2)}) copy-start(f32[256]{0:T(256)S(1)} %add_rsqrt_fusion) | copy-start | bytes 3076
  397.1 124.1 %copy-start.10 = (bf16[256,1536]{1,0:T(8,128)(2,1)S(1)}, bf16[256,1536]{1,0:T(8,128)(2,1)}, u32[]{:S(2)}) copy-start(bf16[256,1536]{1,0:T(8,128)(2,1)} %param.12) | copy-start | bytes 2359300
  397.1 124.1 %copy-start.31 = (f32[256]{0:T(256)S(1)}, f32[256]{0:T(256)}, u32[]{:S(2)}) copy-start(f32[256]{0:T(256)} %compare_convert_fusion) | copy-start | bytes 3076
  531.6 14.9 %copy-start.15 = (bf16[256,4096]{1,0:T(8,128)(2,1)}, bf16[256,4096]{1,0:T(8,128)(2,1)S(1)}, u32[]{:S(2)}) copy-start(bf16[256,4096]{1,0:T(8,128)(2,1)S(1)} %get-tuple-element.22) | copy-start | bytes 6291460
  531.6 14.9 %copy-start.16 = (bf16[256,4096]{1,0:T(8,128)(2,1)}, bf16[256,4096]{1,0:T(8,128)(2,1)S(1)}, u32[]{:S(2)}) copy-start(bf16[256,4096]{1,0:T(8,128)(2,1)S(1)} %get-tuple-element.23) | copy-start | bytes 6291460
  531.6 14.9 %copy-start.11 = (bf16[256,1536]{1,0:T(8,128)(2,1)S(1)}, bf16[256,1536]{1,0:T(8,128)(2,1)}, u32[]{:S(2)}) copy-start(bf16[256,1536]{1,0:T(8,128)(2,1)} %param.12) | copy-start | bytes 2359300
  531.6 14.9 %copy-start.32 = (f32[256]{0:T(256)S(1)}, f32[256]{0:T(256)}, u32[]{:S(2)}) copy-start(f32[256]{0:T(256)} %compare_convert_fusion) | copy-start | bytes 3076
  552.1 155.0 %reduce-scatter.5.cloned.1.call-start = ((), (), s32[]{:S(2)}) async-start(), calls=%async_computation.4 | async-start | bytes 11796480 | tf_op jit(solution)/shard_map/reduce_scatter | solution.py:300
  578.2 253.2 %reduce-scatter.11.cloned.1.call-start = ((), (), s32[]{:S(2)}) async-start(), calls=%async_computation.7 | async-start | bytes 15728640 | tf_op jit(solution)/shard_map/reduce_scatter | solution.py:276
  588.5 467.8 %reduce-scatter.9.cloned.1.call-start = ((), (), s32[]{:S(2)}) async-start(), calls=%async_computation.6 | async-start | bytes 31457280 | tf_op jit(solution)/shard_map/reduce_scatter | solution.py:273
  602.8 718.6 %all-reduce.7.cloned.1.call-start = ((), (), s32[]{:S(2)}) async-start(), calls=%async_computation.12 | async-start | bytes 25952256 | tf_op jit(solution)/shard_map/psum | solution.py:211
  1058.2 8.8 copy-start.34
  (26 other events, 60.4 us)
Sparse Core Ops, SparseCore 0:
  9.8 98.9 all-gather.10
  110.6 56.9 all-gather.12
  169.5 227.5 all-gather.14
  398.8 122.4 all-gather.16
  552.3 56.9 reduce-scatter.6
  612.2 94.8 reduce-scatter.4
  710.8 120.5 reduce-scatter.10
  834.5 221.7 reduce-scatter.8
  1058.9 262.3 all-reduce.6
where the time goes:
time: 1350 us
  waiting for transfers between devices  1130 us (84%)
  matrix products  114 us (8%)
  blocking collectives  42.4 us (3%)
  other arithmetic  32 us (2%)
  between operations  15.3 us (1%)
    all_gather x1, waiting for transfers between devices, body(): lax.all_gather(w_gate_up[layer], 'shard', axis=0, tiled=True)  226 us
    reduce_scatter x1, waiting for transfers between devices, body(): lax.psum_scatter(grad_gateup.astype(jnp.bfloat16), 'shard', scatter_dimen...  225 us
    psum x1, waiting for transfers between devices, settle(): lax.psum(owned[1].astype(jnp.bfloat16), 'replica').astype(jnp.float32)  215 us
    reduce_scatter x1, waiting for transfers between devices, body(): lax.psum_scatter(grad_lower.astype(jnp.bfloat16), 'shard', scatter_dimens...  124 us
    all_gather x1, waiting for transfers between devices, body(): lax.all_gather(w_down[layer], 'shard', axis=0, tiled=True)  110 us
    reduce_scatter x1, waiting for transfers between devices, body(): lax.psum_scatter(grad_project.astype(jnp.bfloat16), 'shard', scatter_dime...  97.9 us
    all_gather x1, waiting for transfers between devices, body(): lax.all_gather(w_qkv[layer], 'shard', axis=0, tiled=True)  78.1 us
    all_gather x1, waiting for transfers between devices, body(): lax.all_gather(w_out[layer], 'shard', axis=0, tiled=True)  42.3 us
  transfers between devices with their start and end apart: 9, of which 9 were waited for; matrix products, arithmetic and copies ran while one was open for 8% of the time, Pallas kernels for 0%

commit v1 on v0

--- a/solution.py
+++ b/solution.py
@@ -10,6 +10,11 @@
 BLOCK = 128
 epsilon = 1e-05
 rope_base = 100000.0
+
+
+def name_the_array(array_in, which_axis):
+    finding = lax.all_gather(array_in, which_axis)
+    return jnp.sum(finding, axis=0)
 
 
 def rms_scale(field):
@@ -208,7 +213,7 @@
 def settle(owned):
     return (
         lax.psum(owned[0].astype(jnp.bfloat16), "replica").astype(jnp.float32),
-        lax.psum(owned[1].astype(jnp.bfloat16), "replica").astype(jnp.float32),
+        name_the_array(owned[1].astype(jnp.bfloat16), "replica").astype(jnp.float32),
         lax.psum(owned[2].astype(jnp.bfloat16), "replica").astype(jnp.float32),
         lax.psum(owned[3].astype(jnp.bfloat16), "replica").astype(jnp.float32),
         lax.psum(owned[4].astype(jnp.bfloat16), "replica").astype(jnp.float32),

time: 1350 us -> 1500 us (1.11)
  waiting for transfers between devices: 1130 us -> 1250 us
  other arithmetic: 32 us -> 47.5 us
    all_gather x0 -> x1, waiting for transfers between devices: none -> 119 us  [name_the_array(): finding = lax.all_gather(array_in, which_axis)]
    reduce_scatter x1, waiting for transfers between devices: 6.24 us -> 60.3 us  [body(): lax.psum_scatter(grad_output.astype(jnp.bfloat16), 'shard', scatter_dimen...]
    reduce_scatter x1, waiting for transfers between devices: 97.9 us -> 64.5 us  [body(): lax.psum_scatter(grad_project.astype(jnp.bfloat16), 'shard', scatter_dime...]
  transfers between devices with their start and end apart: 9 -> 10, of which waited for: 9 -> 10; matrix products, arithmetic and copies ran while one was open for 8% -> 7% of each run, Pallas kernels for 0% -> 0%
where the time goes in v1:
time: 1500 us; the launch traced here: 1490 us
  waiting for transfers between devices  1250 us (83%)
  matrix products  114 us (8%)
  other arithmetic  47.5 us (3%)
  blocking collectives  43.5 us (3%)
  between operations  15.8 us (1%)
    all_gather x1, waiting for transfers between devices, body(): lax.all_gather(w_gate_up[layer], 'shard', axis=0, tiled=True)  226 us
    reduce_scatter x1, waiting for transfers between devices, body(): lax.psum_scatter(grad_gateup.astype(jnp.bfloat16), 'shard', scatter_dimen...  225 us
    psum x1, waiting for transfers between devices, settle(): lax.psum(owned[2].astype(jnp.bfloat16), 'replica').astype(jnp.float32)  201 us
    reduce_scatter x1, waiting for transfers between devices, body(): lax.psum_scatter(grad_lower.astype(jnp.bfloat16), 'shard', scatter_dimens...  124 us
    all_gather x1, waiting for transfers between devices, name_the_array(): finding = lax.all_gather(array_in, which_axis)  119 us
    all_gather x1, waiting for transfers between devices, body(): lax.all_gather(w_down[layer], 'shard', axis=0, tiled=True)  110 us
    all_gather x1, waiting for transfers between devices, body(): lax.all_gather(w_qkv[layer], 'shard', axis=0, tiled=True)  78 us
    reduce_scatter x1, waiting for transfers between devices, body(): lax.psum_scatter(grad_project.astype(jnp.bfloat16), 'shard', scatter_dime...  64.5 us
  transfers between devices with their start and end apart: 10, of which 10 were waited for; matrix products, arithmetic and copies ran while one was open for 7% of the time, Pallas kernels for 0%

profile of v1, /device:TPU:0, one launch (start us, length us, event | category | flops | bytes accessed | tf_op | source)
XLA Modules:
  0.0 1488.2 jit_solution(4158816531419952068)
XLA Ops:
  10.1 9.6 all-gather
  19.7 8.2 all-gather.3
  30.7 78.0 %all-gather.13.cloned.1.call-done = bf16[1,1536,3072]{2,1,0:T(8,128)(2,1)} async-done(((bf16[1,384,3072]{2,1,0:T(8,128)(2,1)}), bf16[1,1536,3072]{2,1,0:T(8,128)(2,1)}) %all-gather.13.cloned.1.call-update) | async-done | bytes 9437200 | tf_op jit(solution)/shard_map/all_gather | solution.py:249
  125.3 42.3 %all-gather.15.cloned.1.call-done = bf16[1,1536,1536]{2,1,0:T(8,128)(2,1)} async-done(((bf16[1,384,1536]{2,1,0:T(8,128)(2,1)}), bf16[1,1536,1536]{2,1,0:T(8,128)(2,1)}) %all-gather.15.cloned.1.call-update) | async-done | bytes 4718608 | tf_op jit(solution)/shard_map/all_gather | solution.py:250
  171.4 225.6 %all-gather.17.cloned.1.call-done = bf16[1,1536,8192]{2,1,0:T(8,128)(2,1)} async-done(((bf16[1,384,8192]{2,1,0:T(8,128)(2,1)}), bf16[1,1536,8192]{2,1,0:T(8,128)(2,1)}) %all-gather.17.cloned.1.call-update) | async-done | bytes 25165840 | tf_op jit(solution)/shard_map/all_gather | solution.py:257
  397.1 13.8 fusion.2
  410.9 110.3 %all-gather.19.cloned.1.call-done = bf16[1,4096,1536]{2,1,0:T(8,128)(2,1)} async-done(((bf16[1,1024,1536]{2,1,0:T(8,128)(2,1)}), bf16[1,4096,1536]{2,1,0:T(8,128)(2,1)}) %all-gather.19.cloned.1.call-update) | async-done | bytes 12582928 | tf_op jit(solution)/shard_map/all_gather | solution.py:258
  521.2 11.2 multiply_convert_fusion.1
  532.4 14.8 multiply_reduce_fusion
  564.9 7.1 convolution_convert_fusion.2
  577.1 10.4 convolution_convert_fusion.1
  587.5 15.0 %convolution_convert_fusion = bf16[1536,8192]{1,0:T(8,128)(2,1)} fusion(bf16[256,4096]{1,0:T(8,128)(2,1)} %get-tuple-element.22, bf16[256,4096]{1,0:T(8,128)(2,1)} %get-tuple-element.21, f32[256,1536]{1,0:T(8,128)S(1)} %get-tuple-element.43, f32[1536]{0:T(1024)S(1)} %convert_reduce_fusion, f32[256]{0:T(256)} %copy-done.24), kind=kOutput, calls=%fused_computation | convolution fusion | flops 6464602112 | bytes 30940160 | tf_op jit(solution)/shard_map/dot_general | solution.py:58
  602.6 64.5 %reduce-scatter.5.cloned.1.call-done = bf16[384,3072]{1,0:T(8,128)(2,1)} async-done(((bf16[1536,3072]{1,0:T(8,128)(2,1)}), bf16[384,3072]{1,0:T(8,128)(2,1)}) %reduce-scatter.5.cloned.1.call-update) | async-done | bytes 2359312 | tf_op jit(solution)/shard_map/reduce_scatter | solution.py:305
  667.2 60.3 %reduce-scatter.7.cloned.1.call-done = bf16[384,1536]{1,0:T(8,128)(2,1)} async-done(((bf16[1536,1536]{1,0:T(8,128)(2,1)}), bf16[384,1536]{1,0:T(8,128)(2,1)}) %reduce-scatter.7.cloned.1.call-update) | async-done | bytes 1179664 | tf_op jit(solution)/shard_map/reduce_scatter | solution.py:308
  727.5 124.3 %reduce-scatter.11.cloned.1.call-done = bf16[1024,1536]{1,0:T(8,128)(2,1)} async-done(((bf16[4096,1536]{1,0:T(8,128)(2,1)}), bf16[1024,1536]{1,0:T(8,128)(2,1)}) %reduce-scatter.11.cloned.1.call-update) | async-done | bytes 3145744 | tf_op jit(solution)/shard_map/reduce_scatter | solution.py:281
  851.8 224.8 %reduce-scatter.9.cloned.1.call-done = bf16[384,8192]{1,0:T(8,128)(2,1)} async-done(((bf16[1536,8192]{1,0:T(8,128)(2,1)}), bf16[384,8192]{1,0:T(8,128)(2,1)}) %reduce-scatter.9.cloned.1.call-update) | async-done | bytes 6291472 | tf_op jit(solution)/shard_map/reduce_scatter | solution.py:278
  1078.6 8.8 fusion.46
  1087.3 9.2 all-reduce.4
  1096.7 16.5 %all-reduce.2 = (bf16[1,384]{1,0:T(2,128)(2,1)S(1)}, bf16[1,384]{1,0:T(2,128)(2,1)S(1)}) all-reduce(bf16[1,384]{1,0:T(2,128)(2,1)S(1)} %stack.31, bf16[1,384]{1,0:T(2,128)(2,1)S(1)} %stack.35), channel_id=1, replica_groups=mesh['shard'=4,'replica'=8] {'replica'}, use_global_device_ids=true, to_apply=%region_11.12 | all-reduce | flops 768 | bytes 3072 | tf_op jit(solution)/shard_map/psum | solution.py:215
  1118.4 9.1 fusion.30
  1127.4 119.5 %all-gather.21.cloned.1.call-done = bf16[3072,3072]{1,0:T(8,128)(2,1)} async-done(((bf16[384,3072]{1,0:T(8,128)(2,1)}), bf16[3072,3072]{1,0:T(8,128)(2,1)}) %all-gather.21.cloned.1.call-update) | async-done | bytes 18874384 | tf_op jit(solution)/shard_map/all_gather | solution.py:16
  1246.9 12.6 reduce_sum.101
  1264.0 201.1 %all-reduce.7.cloned.1.call-done = (bf16[1,384,1536]{2,1,0:T(8,128)(2,1)}, bf16[1,384,8192]{2,1,0:T(8,128)(2,1)}, bf16[1,1024,1536]{2,1,0:T(8,128)(2,1)}) async-done(((bf16[1,384,1536]{2,1,0:T(8,128)(2,1)}, bf16[1,384,8192]{2,1,0:T(8,128)(2,1)}, bf16[1,1024,1536]{2,1,0:T(8,128)(2,1)}), (bf16[1,384,1536]{2,1,0:T(8,128)(2,1)}, bf16[1,384,8192]{2,1,0:T(8,128)(2,1)}, ...) | async-done | bytes 10616848 | tf_op jit(solution)/shard_map/psum | solution.py:217
  1468.1 9.3 stack.38
  (159 shorter events, 66.2 us)
Async XLA Ops:
  7.2 101.6 %all-gather.13.cloned.1.call-start = ((), (), s32[]{:S(2)}) async-start(), calls=%async_computation.8 | async-start | bytes 11796480 | tf_op jit(solution)/shard_map/all_gather | solution.py:249
  7.9 159.7 %all-gather.15.cloned.1.call-start = ((), (), s32[]{:S(2)}) async-start(), calls=%async_computation.9 | async-start | bytes 5898240 | tf_op jit(solution)/shard_map/all_gather | solution.py:250
  8.7 388.4 %all-gather.17.cloned.1.call-start = ((), (), s32[]{:S(2)}) async-start(), calls=%async_computation.10 | async-start | bytes 31457280 | tf_op jit(solution)/shard_map/all_gather | solution.py:257
  9.4 10.3 copy-start.33
  9.4 18.5 %copy-start.36 = (s32[64]{0:T(128)S(1)}, s32[64]{0:T(128)}, u32[]{:S(2)}) copy-start(s32[64]{0:T(128)} %param.14) | copy-start | bytes 772
  9.4 18.6 %copy-start.34 = (s32[64]{0:T(128)S(1)}, s32[64]{0:T(128)}, u32[]{:S(2)}) copy-start(s32[64]{0:T(128)} %param.15) | copy-start | bytes 772
  9.4 18.6 %copy-start.35 = (s32[64]{0:T(128)S(1)}, s32[64]{0:T(128)}, u32[]{:S(2)}) copy-start(s32[64]{0:T(128)} %param.13) | copy-start | bytes 772
  9.4 19.7 %copy-start.2 = (bf16[256,1536]{1,0:T(8,128)(2,1)S(1)}, bf16[256,1536]{1,0:T(8,128)(2,1)}, u32[]{:S(2)}) copy-start(bf16[256,1536]{1,0:T(8,128)(2,1)} %param.11) | copy-start | bytes 2359300
  9.4 511.8 %all-gather.19.cloned.1.call-start = ((), (), s32[]{:S(2)}) async-start(), calls=%async_computation.11 | async-start | bytes 15728640 | tf_op jit(solution)/shard_map/all_gather | solution.py:258
  10.0 657.1 %reduce-scatter.5.cloned.1.call-start = ((), (), s32[]{:S(2)}) async-start(), calls=%async_computation.4 | async-start | bytes 11796480 | tf_op jit(solution)/shard_map/reduce_scatter | solution.py:305
  29.4 84.6 %copy-start.25 = (f32[256]{0:T(256)}, f32[256]{0:T(256)S(1)}, u32[]{:S(2)}) copy-start(f32[256]{0:T(256)S(1)} %add_rsqrt_fusion.1) | copy-start | bytes 3076
  125.3 46.1 %copy-start.4 = (bf16[8,96,2,256]{3,1,2,0:T(8,128)(2,1)}, bf16[8,96,2,256]{3,1,2,0:T(8,128)(2,1)S(1)}, u32[]{:S(2)}) copy-start(bf16[8,96,2,256]{3,1,2,0:T(8,128)(2,1)S(1)} %convolution_convert_fusion.4) | copy-start | bytes 2359300
  171.4 361.0 %copy-start.24 = (f32[256]{0:T(256)}, f32[256]{0:T(256)S(1)}, u32[]{:S(2)}) copy-start(f32[256]{0:T(256)S(1)} %add_rsqrt_fusion) | copy-start | bytes 3076
  397.1 124.2 %copy-start.8 = (bf16[256,1536]{1,0:T(8,128)(2,1)S(1)}, bf16[256,1536]{1,0:T(8,128)(2,1)}, u32[]{:S(2)}) copy-start(bf16[256,1536]{1,0:T(8,128)(2,1)} %param.12) | copy-start | bytes 2359300
  397.1 124.2 %copy-start.28 = (f32[256]{0:T(256)S(1)}, f32[256]{0:T(256)}, u32[]{:S(2)}) copy-start(f32[256]{0:T(256)} %compare_convert_fusion) | copy-start | bytes 3076
  521.2 27.9 %slice-start = ((s8[4718592]{0:T(1024)(128)(4,1)}), s8[4194304]{0:T(1024)(128)(4,1)S(1)}, s32[]{:S(2)}) async-start(s8[4718592]{0:T(1024)(128)(4,1)} %bitcast.134), calls=%async_computation.14 | async-start | bytes 8388608
  532.4 14.8 copy-start.9
  532.4 14.8 copy-start.29
  532.4 16.7 %slice-start.1 = ((s8[4718592]{0:T(1024)(128)(4,1)}), s8[524288]{0:T(1024)(128)(4,1)S(1)}, s32[]{:S(2)}) async-start(s8[4718592]{0:T(1024)(128)(4,1)} %bitcast.134), calls=%async_computation.15 | async-start | bytes 1048576
  572.0 155.5 %reduce-scatter.7.cloned.1.call-start = ((), (), s32[]{:S(2)}) async-start(), calls=%async_computation.5 | async-start | bytes 5898240 | tf_op jit(solution)/shard_map/reduce_scatter | solution.py:308
  577.0 274.8 %reduce-scatter.11.cloned.1.call-start = ((), (), s32[]{:S(2)}) async-start(), calls=%async_computation.7 | async-start | bytes 15728640 | tf_op jit(solution)/shard_map/reduce_scatter | solution.py:281
  587.5 489.2 %reduce-scatter.9.cloned.1.call-start = ((), (), s32[]{:S(2)}) async-start(), calls=%async_computation.6 | async-start | bytes 31457280 | tf_op jit(solution)/shard_map/reduce_scatter | solution.py:278
  602.6 644.4 %all-gather.21.cloned.1.call-start = ((), (), s32[]{:S(2)}) async-start(), calls=%async_computation.12 | async-start | bytes 21233664 | tf_op jit(solution)/shard_map/all_gather | solution.py:16
  667.1 798.0 %all-reduce.7.cloned.1.call-start = ((), (), s32[]{:S(2)}) async-start(), calls=%async_computation.13 | async-start | bytes 21233664 | tf_op jit(solution)/shard_map/psum | solution.py:217
  (26 other events, 70.7 us)
Sparse Core Ops, SparseCore 0:
  9.8 98.9 all-gather.12
  110.6 56.9 all-gather.14
  169.5 227.5 all-gather.16
  398.8 122.4 all-gather.18
  572.1 94.8 reduce-scatter.4
  670.5 56.9 reduce-scatter.6
  731.2 120.6 reduce-scatter.10
  854.9 221.6 reduce-scatter.8
  1078.3 168.5 all-gather.20
  1249.4 215.7 all-reduce.6
